TPU v7x, 8 devices: a whole 2x2x1 slice. The times are simulated.
8 devices in a mesh: dp: 1 (over z), tp: 2 (over y), pp: 4 (over x, core).
Axes of the slice: x: 2, y: 2, z: 1, core: 2. Of those that a mesh axis runs over, the one named last changes fastest.
Arguments:
- hidden_in: bfloat16 [8, 1, 768, 2048], P('dp', None, 'tp')
- norm_gains: float32 [4, 4, 2048], P('pp')
- w_query: bfloat16 [4, 2048, 8, 256], P('pp', None, 'tp')
- w_key: bfloat16 [4, 2048, 2, 256], P('pp')
- w_value: bfloat16 [4, 2048, 2, 256], P('pp')
- w_out: bfloat16 [4, 8, 256, 2048], P('pp', 'tp')
- w_gate: bfloat16 [4, 2048, 16384], P('pp', None, 'tp')
- w_up: bfloat16 [4, 2048, 16384], P('pp', None, 'tp')
- w_down: bfloat16 [4, 16384, 2048], P('pp', 'tp')
Outputs:
- output: bfloat16 [8, 1, 768, 2048], P('dp', None, ('tp', 'pp'))
All inputs are finite; a program needn't handle non-finite values.
Results may differ from a plain program's by a relative error of at most 0.02.
Values are sent between devices in bfloat16 or wider.
A program may use at most 1 GiB of HBM per device.

v0:
```python
import jax
import jax.numpy as jnp
from jax import lax
from jax.sharding import PartitionSpec as P

WINDOW = 512
SOFTCAP = 50.0
ROPE_BASE = 10000.0
NORM_EPS = 1e-6


def rms_scale(values, gain):
    as_f32 = values.astype(jnp.float32)
    mean_sq = jnp.mean(as_f32 * as_f32, axis=-1, keepdims=True)
    return (as_f32 * lax.rsqrt(mean_sq + NORM_EPS) * (1.0 + gain)).astype(jnp.bfloat16)


def add_norm(residual, branch, gain):
    return (residual.astype(jnp.float32) + rms_scale(branch, gain).astype(jnp.float32)).astype(jnp.bfloat16)


def apply_rope(projected):
    seq_len, head_dim = projected.shape[1], projected.shape[3]
    half_dim = head_dim // 2
    frequency = jnp.power(ROPE_BASE, -2.0 * jnp.arange(half_dim, dtype=jnp.float32) / head_dim)
    angle = jnp.arange(seq_len, dtype=jnp.float32)[:, None] * frequency[None, :]
    cos_t = jnp.cos(angle)[None, :, None, :]
    sin_t = jnp.sin(angle)[None, :, None, :]
    first = projected[..., :half_dim]
    second = projected[..., half_dim:]
    return jnp.concatenate([first * cos_t - second * sin_t, second * cos_t + first * sin_t], axis=-1).astype(jnp.bfloat16)


def attend(query, keys, values, window):
    batch, seq_len, q_heads, head_dim = query.shape
    kv_heads = keys.shape[2]
    grouped = query.reshape(batch, seq_len, kv_heads, q_heads // kv_heads, head_dim)
    q_block = min(seq_len, 256)
    key_len = min(seq_len, window + q_block) if window > 0 else seq_len
    scale = head_dim ** -0.5

    def one_block(start):
        key_start = jnp.clip(start + q_block - key_len, 0, seq_len - key_len)
        q_part = lax.dynamic_slice_in_dim(grouped, start, q_block, axis=1)
        k_part = lax.dynamic_slice_in_dim(keys, key_start, key_len, axis=1)
        v_part = lax.dynamic_slice_in_dim(values, key_start, key_len, axis=1)
        scores = jnp.einsum('bqkgd,bskd->bkgqs', q_part, k_part, preferred_element_type=jnp.float32) * scale
        scores = SOFTCAP * jnp.tanh(scores / SOFTCAP)
        offset = (start + jnp.arange(q_block))[:, None] - (key_start + jnp.arange(key_len))[None, :]
        allowed = offset >= 0
        if window > 0:
            allowed = allowed & (offset < window)
        scores = jnp.where(allowed, scores, -1e30)
        attn_prob = jax.nn.softmax(scores, axis=-1).astype(jnp.bfloat16)
        return jnp.einsum('bkgqs,bskd->bqkgd', attn_prob, v_part, preferred_element_type=jnp.float32).astype(jnp.bfloat16)

    starts = jnp.arange(seq_len // q_block) * q_block
    blocks = lax.map(one_block, starts)
    return jnp.moveaxis(blocks, 0, 1).reshape(batch, seq_len, q_heads, head_dim)


def local_attend(query, keys, values):
    return attend(query, keys, values, WINDOW)


def global_attend(query, keys, values):
    return attend(query, keys, values, 0)


def head_weights(w_key_all, w_value_all, tp_size, q_heads):
    kv_total = w_key_all.shape[1]
    kv_local = max(kv_total // tp_size, 1)
    group = (q_heads * tp_size) // kv_total
    kv_start = (lax.axis_index('tp') * q_heads) // group
    return (lax.dynamic_slice_in_dim(w_key_all, kv_start, kv_local, axis=1),
            lax.dynamic_slice_in_dim(w_value_all, kv_start, kv_local, axis=1))


def solution(mesh):
    tp_size = mesh.shape['tp']
    stages = mesh.shape['pp']
    in_specs = (P('dp', None, 'tp', None), P('pp', None, None), P('pp', None, 'tp', None),
                P('pp', None, None, None), P('pp', None, None, None), P('pp', 'tp', None, None),
                P('pp', None, 'tp'), P('pp', None, 'tp'), P('pp', 'tp', None))
    out_spec = P('dp', None, ('tp', 'pp'), None)
    forward_send = [(source, source + 1) for source in range(stages - 1)]

    def stage_program(hidden_in, norm_gains, w_query, w_key, w_value, w_out, w_gate, w_up, w_down):
        stage = lax.axis_index('pp')
        micro = hidden_in.shape[0]
        gains = norm_gains[0]
        w_q = w_query[0]
        w_o = w_out[0]
        w_g = w_gate[0]
        w_u = w_up[0]
        w_d = w_down[0]
        w_k, w_v = head_weights(w_key[0], w_value[0], tp_size, w_q.shape[1])

        def run_layer(residual):
            normed = rms_scale(residual, gains[0])
            gathered = lax.all_gather(normed, 'tp', axis=1, tiled=True)
            query = apply_rope(jnp.einsum('btd,dhk->bthk', gathered, w_q, preferred_element_type=jnp.float32))
            keys = apply_rope(jnp.einsum('btd,dhk->bthk', gathered, w_k, preferred_element_type=jnp.float32))
            values = jnp.einsum('btd,dhk->bthk', gathered, w_v, preferred_element_type=jnp.float32).astype(jnp.bfloat16)
            mixed = lax.cond(stage % 2 == 0, local_attend, global_attend, query, keys, values)
            part_sum = jnp.einsum('bthk,hkd->btd', mixed, w_o, preferred_element_type=jnp.float32).astype(jnp.bfloat16)
            attn_proj = lax.psum_scatter(part_sum, 'tp', scatter_dimension=1, tiled=True)
            residual = add_norm(residual, attn_proj, gains[1])
            normed = rms_scale(residual, gains[2])
            gathered = lax.all_gather(normed, 'tp', axis=1, tiled=True)
            gate_proj = jnp.einsum('btd,df->btf', gathered, w_g, preferred_element_type=jnp.float32)
            up_proj = jnp.einsum('btd,df->btf', gathered, w_u, preferred_element_type=jnp.float32)
            hidden = (jax.nn.gelu(gate_proj, approximate=True) * up_proj).astype(jnp.bfloat16)
            part_sum = jnp.einsum('btf,fd->btd', hidden, w_d, preferred_element_type=jnp.float32).astype(jnp.bfloat16)
            down_proj = lax.psum_scatter(part_sum, 'tp', scatter_dimension=1, tiled=True)
            return add_norm(residual, down_proj, gains[3])

        def step_body(step, carry):
            incoming, out_buf = carry
            fresh = lax.dynamic_index_in_dim(hidden_in, jnp.minimum(step, micro - 1), axis=0, keepdims=False)
            result = run_layer(jnp.where(stage == 0, fresh, incoming))
            slot = jnp.clip(step - (stages - 1), 0, micro - 1)
            kept = lax.dynamic_index_in_dim(out_buf, slot, axis=0, keepdims=False)
            stored = jnp.where(step >= stages - 1, result, kept)
            out_buf = lax.dynamic_update_slice_in_dim(out_buf, stored[None], slot, axis=0)
            return lax.ppermute(result, 'pp', forward_send), out_buf

        initial = (jnp.zeros_like(hidden_in[0]), jnp.zeros_like(hidden_in))
        _, out_buf = lax.fori_loop(0, micro + stages - 1, step_body, initial)
        finished = jnp.where(stage == stages - 1, out_buf, jnp.zeros_like(out_buf))
        return lax.psum_scatter(finished, 'pp', scatter_dimension=2, tiled=True)

    return jax.shard_map(stage_program, mesh=mesh, in_specs=in_specs, out_specs=out_spec, check_vma=False)
```

profile of v0, /device:TPU:7, one launch (start us, length us, event | category | flops | bytes accessed | tf_op | source)
XLA Modules:
  0.0 4196.2 jit_solution(1643324832025665276)
XLA Ops:
  29.4 4047.6 %while.45 = (s32[]{:T(128)}, bf16[1,384,2048]{2,1,0:T(8,128)(2,1)S(1)}, bf16[8,1,384,2048]{3,2,1,0:T(8,128)(2,1)}, pred[]{:T(512)}, bf16[8,1,384,2048]{3,2,1,0:T...) while((s32[]{:T(128)}, ...), condition=%wide.region_17.18_spmd, body=%wide.region_0.17_spmd.sunk | while | flops 86280118272 | bytes 403364384 | solution.py:129
  179.7 42.3 %all-gather.5.cloned.1.call-done = bf16[1,768,2048]{2,1,0:T(8,128)(2,1)} async-done(((bf16[1,384,2048]{2,1,0:T(8,128)(2,1)}), bf16[1,768,2048]{2,1,0:T(8,128)(2,1)}) %all-gather.5.cloned.1.call-update) | async-done | bytes 3145744 | tf_op jit(solution)/shard_map/while/body/eval_jaxpr/all_gather | solution.py:110
  389.1 56.8 %all-gather.3.cloned.1.call-done = bf16[1,768,2048]{2,1,0:T(8,128)(2,1)} async-done(((bf16[1,384,2048]{2,1,0:T(8,128)(2,1)}), bf16[1,768,2048]{2,1,0:T(8,128)(2,1)}) %all-gather.3.cloned.1.call-update) | async-done | bytes 3145744 | tf_op jit(solution)/shard_map/while/body/eval_jaxpr/all_gather | solution.py:101
  549.1 42.3 %all-gather.5.cloned.1.call-done = bf16[1,768,2048]{2,1,0:T(8,128)(2,1)} async-done(((bf16[1,384,2048]{2,1,0:T(8,128)(2,1)}), bf16[1,768,2048]{2,1,0:T(8,128)(2,1)}) %all-gather.5.cloned.1.call-update) | async-done | bytes 3145744 | tf_op jit(solution)/shard_map/while/body/eval_jaxpr/all_gather | solution.py:110
  758.4 56.8 %all-gather.3.cloned.1.call-done = bf16[1,768,2048]{2,1,0:T(8,128)(2,1)} async-done(((bf16[1,384,2048]{2,1,0:T(8,128)(2,1)}), bf16[1,768,2048]{2,1,0:T(8,128)(2,1)}) %all-gather.3.cloned.1.call-update) | async-done | bytes 3145744 | tf_op jit(solution)/shard_map/while/body/eval_jaxpr/all_gather | solution.py:101
  918.3 42.3 %all-gather.5.cloned.1.call-done = bf16[1,768,2048]{2,1,0:T(8,128)(2,1)} async-done(((bf16[1,384,2048]{2,1,0:T(8,128)(2,1)}), bf16[1,768,2048]{2,1,0:T(8,128)(2,1)}) %all-gather.5.cloned.1.call-update) | async-done | bytes 3145744 | tf_op jit(solution)/shard_map/while/body/eval_jaxpr/all_gather | solution.py:110
  1127.5 56.8 %all-gather.3.cloned.1.call-done = bf16[1,768,2048]{2,1,0:T(8,128)(2,1)} async-done(((bf16[1,384,2048]{2,1,0:T(8,128)(2,1)}), bf16[1,768,2048]{2,1,0:T(8,128)(2,1)}) %all-gather.3.cloned.1.call-update) | async-done | bytes 3145744 | tf_op jit(solution)/shard_map/while/body/eval_jaxpr/all_gather | solution.py:101
  1240.1 40.6 reduce-scatter.6.cloned.1.call-done
  1287.7 42.3 %all-gather.5.cloned.1.call-done = bf16[1,768,2048]{2,1,0:T(8,128)(2,1)} async-done(((bf16[1,384,2048]{2,1,0:T(8,128)(2,1)}), bf16[1,768,2048]{2,1,0:T(8,128)(2,1)}) %all-gather.5.cloned.1.call-update) | async-done | bytes 3145744 | tf_op jit(solution)/shard_map/while/body/eval_jaxpr/all_gather | solution.py:110
  1497.0 56.8 %all-gather.3.cloned.1.call-done = bf16[1,768,2048]{2,1,0:T(8,128)(2,1)} async-done(((bf16[1,384,2048]{2,1,0:T(8,128)(2,1)}), bf16[1,768,2048]{2,1,0:T(8,128)(2,1)}) %all-gather.3.cloned.1.call-update) | async-done | bytes 3145744 | tf_op jit(solution)/shard_map/while/body/eval_jaxpr/all_gather | solution.py:101
  1657.0 42.3 %all-gather.5.cloned.1.call-done = bf16[1,768,2048]{2,1,0:T(8,128)(2,1)} async-done(((bf16[1,384,2048]{2,1,0:T(8,128)(2,1)}), bf16[1,768,2048]{2,1,0:T(8,128)(2,1)}) %all-gather.5.cloned.1.call-update) | async-done | bytes 3145744 | tf_op jit(solution)/shard_map/while/body/eval_jaxpr/all_gather | solution.py:110
  1866.2 56.8 %all-gather.3.cloned.1.call-done = bf16[1,768,2048]{2,1,0:T(8,128)(2,1)} async-done(((bf16[1,384,2048]{2,1,0:T(8,128)(2,1)}), bf16[1,768,2048]{2,1,0:T(8,128)(2,1)}) %all-gather.3.cloned.1.call-update) | async-done | bytes 3145744 | tf_op jit(solution)/shard_map/while/body/eval_jaxpr/all_gather | solution.py:101
  2026.2 42.3 %all-gather.5.cloned.1.call-done = bf16[1,768,2048]{2,1,0:T(8,128)(2,1)} async-done(((bf16[1,384,2048]{2,1,0:T(8,128)(2,1)}), bf16[1,768,2048]{2,1,0:T(8,128)(2,1)}) %all-gather.5.cloned.1.call-update) | async-done | bytes 3145744 | tf_op jit(solution)/shard_map/while/body/eval_jaxpr/all_gather | solution.py:110
  2235.4 56.8 %all-gather.3.cloned.1.call-done = bf16[1,768,2048]{2,1,0:T(8,128)(2,1)} async-done(((bf16[1,384,2048]{2,1,0:T(8,128)(2,1)}), bf16[1,768,2048]{2,1,0:T(8,128)(2,1)}) %all-gather.3.cloned.1.call-update) | async-done | bytes 3145744 | tf_op jit(solution)/shard_map/while/body/eval_jaxpr/all_gather | solution.py:101
  2395.6 42.3 %all-gather.5.cloned.1.call-done = bf16[1,768,2048]{2,1,0:T(8,128)(2,1)} async-done(((bf16[1,384,2048]{2,1,0:T(8,128)(2,1)}), bf16[1,768,2048]{2,1,0:T(8,128)(2,1)}) %all-gather.5.cloned.1.call-update) | async-done | bytes 3145744 | tf_op jit(solution)/shard_map/while/body/eval_jaxpr/all_gather | solution.py:110
  2604.9 56.8 %all-gather.3.cloned.1.call-done = bf16[1,768,2048]{2,1,0:T(8,128)(2,1)} async-done(((bf16[1,384,2048]{2,1,0:T(8,128)(2,1)}), bf16[1,768,2048]{2,1,0:T(8,128)(2,1)}) %all-gather.3.cloned.1.call-update) | async-done | bytes 3145744 | tf_op jit(solution)/shard_map/while/body/eval_jaxpr/all_gather | solution.py:101
  2764.8 42.3 %all-gather.5.cloned.1.call-done = bf16[1,768,2048]{2,1,0:T(8,128)(2,1)} async-done(((bf16[1,384,2048]{2,1,0:T(8,128)(2,1)}), bf16[1,768,2048]{2,1,0:T(8,128)(2,1)}) %all-gather.5.cloned.1.call-update) | async-done | bytes 3145744 | tf_op jit(solution)/shard_map/while/body/eval_jaxpr/all_gather | solution.py:110
  2974.1 56.8 %all-gather.3.cloned.1.call-done = bf16[1,768,2048]{2,1,0:T(8,128)(2,1)} async-done(((bf16[1,384,2048]{2,1,0:T(8,128)(2,1)}), bf16[1,768,2048]{2,1,0:T(8,128)(2,1)}) %all-gather.3.cloned.1.call-update) | async-done | bytes 3145744 | tf_op jit(solution)/shard_map/while/body/eval_jaxpr/all_gather | solution.py:101
  3134.1 42.3 %all-gather.5.cloned.1.call-done = bf16[1,768,2048]{2,1,0:T(8,128)(2,1)} async-done(((bf16[1,384,2048]{2,1,0:T(8,128)(2,1)}), bf16[1,768,2048]{2,1,0:T(8,128)(2,1)}) %all-gather.5.cloned.1.call-update) | async-done | bytes 3145744 | tf_op jit(solution)/shard_map/while/body/eval_jaxpr/all_gather | solution.py:110
  3343.2 56.8 %all-gather.3.cloned.1.call-done = bf16[1,768,2048]{2,1,0:T(8,128)(2,1)} async-done(((bf16[1,384,2048]{2,1,0:T(8,128)(2,1)}), bf16[1,768,2048]{2,1,0:T(8,128)(2,1)}) %all-gather.3.cloned.1.call-update) | async-done | bytes 3145744 | tf_op jit(solution)/shard_map/while/body/eval_jaxpr/all_gather | solution.py:101
  3503.4 42.3 %all-gather.5.cloned.1.call-done = bf16[1,768,2048]{2,1,0:T(8,128)(2,1)} async-done(((bf16[1,384,2048]{2,1,0:T(8,128)(2,1)}), bf16[1,768,2048]{2,1,0:T(8,128)(2,1)}) %all-gather.5.cloned.1.call-update) | async-done | bytes 3145744 | tf_op jit(solution)/shard_map/while/body/eval_jaxpr/all_gather | solution.py:110
  3712.7 56.8 %all-gather.3.cloned.1.call-done = bf16[1,768,2048]{2,1,0:T(8,128)(2,1)} async-done(((bf16[1,384,2048]{2,1,0:T(8,128)(2,1)}), bf16[1,768,2048]{2,1,0:T(8,128)(2,1)}) %all-gather.3.cloned.1.call-update) | async-done | bytes 3145744 | tf_op jit(solution)/shard_map/while/body/eval_jaxpr/all_gather | solution.py:101
  3872.7 42.3 %all-gather.5.cloned.1.call-done = bf16[1,768,2048]{2,1,0:T(8,128)(2,1)} async-done(((bf16[1,384,2048]{2,1,0:T(8,128)(2,1)}), bf16[1,768,2048]{2,1,0:T(8,128)(2,1)}) %all-gather.5.cloned.1.call-update) | async-done | bytes 3145744 | tf_op jit(solution)/shard_map/while/body/eval_jaxpr/all_gather | solution.py:110
  4087.6 101.3 %reduce-scatter.4.cloned.1.call-done = bf16[8,1,96,2048]{3,2,1,0:T(8,128)(2,1)} async-done(((bf16[8,1,384,2048]{3,2,1,0:T(8,128)(2,1)}), bf16[8,1,96,2048]{3,2,1,0:T(8,128)(2,1)}) %reduce-scatter.4.cloned.1.call-update) | async-done | bytes 3145744 | tf_op jit(solution)/shard_map/reduce_scatter | solution.py:131
  (1034 shorter events, 3591.6 us)
Async XLA Ops:
  34.1 138.7 %reduce-scatter.6.cloned.1.call-start = ((), (), s32[]{:S(2)}) async-start(), calls=%async_computation.5 | async-start | bytes 4718592 | tf_op jit(solution)/shard_map/while/body/eval_jaxpr/reduce_scatter | solution.py:107
  179.7 191.0 %reduce-scatter.8.cloned.1.call-start = ((), (), s32[]{:S(2)}) async-start(), calls=%async_computation.7 | async-start | bytes 4718592 | tf_op jit(solution)/shard_map/while/body/eval_jaxpr/reduce_scatter | solution.py:115
  387.6 154.6 %reduce-scatter.6.cloned.1.call-start = ((), (), s32[]{:S(2)}) async-start(), calls=%async_computation.5 | async-start | bytes 4718592 | tf_op jit(solution)/shard_map/while/body/eval_jaxpr/reduce_scatter | solution.py:107
  549.0 191.2 %reduce-scatter.8.cloned.1.call-start = ((), (), s32[]{:S(2)}) async-start(), calls=%async_computation.7 | async-start | bytes 4718592 | tf_op jit(solution)/shard_map/while/body/eval_jaxpr/reduce_scatter | solution.py:115
  756.9 154.6 %reduce-scatter.6.cloned.1.call-start = ((), (), s32[]{:S(2)}) async-start(), calls=%async_computation.5 | async-start | bytes 4718592 | tf_op jit(solution)/shard_map/while/body/eval_jaxpr/reduce_scatter | solution.py:107
  918.3 191.0 %reduce-scatter.8.cloned.1.call-start = ((), (), s32[]{:S(2)}) async-start(), calls=%async_computation.7 | async-start | bytes 4718592 | tf_op jit(solution)/shard_map/while/body/eval_jaxpr/reduce_scatter | solution.py:115
  1126.0 154.8 %reduce-scatter.6.cloned.1.call-start = ((), (), s32[]{:S(2)}) async-start(), calls=%async_computation.5 | async-start | bytes 4718592 | tf_op jit(solution)/shard_map/while/body/eval_jaxpr/reduce_scatter | solution.py:107
  1287.6 191.0 %reduce-scatter.8.cloned.1.call-start = ((), (), s32[]{:S(2)}) async-start(), calls=%async_computation.7 | async-start | bytes 4718592 | tf_op jit(solution)/shard_map/while/body/eval_jaxpr/reduce_scatter | solution.py:115
  1495.5 154.5 %reduce-scatter.6.cloned.1.call-start = ((), (), s32[]{:S(2)}) async-start(), calls=%async_computation.5 | async-start | bytes 4718592 | tf_op jit(solution)/shard_map/while/body/eval_jaxpr/reduce_scatter | solution.py:107
  1656.9 191.2 %reduce-scatter.8.cloned.1.call-start = ((), (), s32[]{:S(2)}) async-start(), calls=%async_computation.7 | async-start | bytes 4718592 | tf_op jit(solution)/shard_map/while/body/eval_jaxpr/reduce_scatter | solution.py:115
  1864.7 154.6 %reduce-scatter.6.cloned.1.call-start = ((), (), s32[]{:S(2)}) async-start(), calls=%async_computation.5 | async-start | bytes 4718592 | tf_op jit(solution)/shard_map/while/body/eval_jaxpr/reduce_scatter | solution.py:107
  2026.1 191.0 %reduce-scatter.8.cloned.1.call-start = ((), (), s32[]{:S(2)}) async-start(), calls=%async_computation.7 | async-start | bytes 4718592 | tf_op jit(solution)/shard_map/while/body/eval_jaxpr/reduce_scatter | solution.py:115
  2233.9 154.8 %reduce-scatter.6.cloned.1.call-start = ((), (), s32[]{:S(2)}) async-start(), calls=%async_computation.5 | async-start | bytes 4718592 | tf_op jit(solution)/shard_map/while/body/eval_jaxpr/reduce_scatter | solution.py:107
  2395.5 191.0 %reduce-scatter.8.cloned.1.call-start = ((), (), s32[]{:S(2)}) async-start(), calls=%async_computation.7 | async-start | bytes 4718592 | tf_op jit(solution)/shard_map/while/body/eval_jaxpr/reduce_scatter | solution.py:115
  2603.3 154.5 %reduce-scatter.6.cloned.1.call-start = ((), (), s32[]{:S(2)}) async-start(), calls=%async_computation.5 | async-start | bytes 4718592 | tf_op jit(solution)/shard_map/while/body/eval_jaxpr/reduce_scatter | solution.py:107
  2764.7 191.2 %reduce-scatter.8.cloned.1.call-start = ((), (), s32[]{:S(2)}) async-start(), calls=%async_computation.7 | async-start | bytes 4718592 | tf_op jit(solution)/shard_map/while/body/eval_jaxpr/reduce_scatter | solution.py:115
  2972.6 154.6 %reduce-scatter.6.cloned.1.call-start = ((), (), s32[]{:S(2)}) async-start(), calls=%async_computation.5 | async-start | bytes 4718592 | tf_op jit(solution)/shard_map/while/body/eval_jaxpr/reduce_scatter | solution.py:107
  3134.0 191.0 %reduce-scatter.8.cloned.1.call-start = ((), (), s32[]{:S(2)}) async-start(), calls=%async_computation.7 | async-start | bytes 4718592 | tf_op jit(solution)/shard_map/while/body/eval_jaxpr/reduce_scatter | solution.py:115
  3341.7 154.8 %reduce-scatter.6.cloned.1.call-start = ((), (), s32[]{:S(2)}) async-start(), calls=%async_computation.5 | async-start | bytes 4718592 | tf_op jit(solution)/shard_map/while/body/eval_jaxpr/reduce_scatter | solution.py:107
  3503.3 191.0 %reduce-scatter.8.cloned.1.call-start = ((), (), s32[]{:S(2)}) async-start(), calls=%async_computation.7 | async-start | bytes 4718592 | tf_op jit(solution)/shard_map/while/body/eval_jaxpr/reduce_scatter | solution.py:115
  3711.2 154.6 %reduce-scatter.6.cloned.1.call-start = ((), (), s32[]{:S(2)}) async-start(), calls=%async_computation.5 | async-start | bytes 4718592 | tf_op jit(solution)/shard_map/while/body/eval_jaxpr/reduce_scatter | solution.py:107
  3824.9 90.0 %all-gather.5.cloned.1.call-start = ((), (), s32[]{:S(2)}) async-start(), calls=%async_computation.6 | async-start | bytes 4718592 | tf_op jit(solution)/shard_map/while/body/eval_jaxpr/all_gather | solution.py:110
  3872.6 191.2 %reduce-scatter.8.cloned.1.call-start = ((), (), s32[]{:S(2)}) async-start(), calls=%async_computation.7 | async-start | bytes 4718592 | tf_op jit(solution)/shard_map/while/body/eval_jaxpr/reduce_scatter | solution.py:115
  4077.0 111.9 %reduce-scatter.4.cloned.1.call-start = ((), (), s32[]{:S(2)}) async-start(), calls=%async_computation.3 | async-start | bytes 15728640 | tf_op jit(solution)/shard_map/reduce_scatter | solution.py:131
  (165 other events, 3947.3 us)
Sparse Core Ops, SparseCore 0:
  34.2 41.8 all-gather.2
  132.1 40.7 reduce-scatter.5
  179.8 42.1 all-gather.4
  387.7 58.1 all-gather.2
  549.1 42.1 all-gather.4
  757.0 58.1 all-gather.2
  918.4 42.1 all-gather.4
  1126.1 58.1 all-gather.2
  1287.7 42.1 all-gather.4
  1495.6 58.1 all-gather.2
  1657.0 42.1 all-gather.4
  1864.8 58.1 all-gather.2
  2026.3 42.1 all-gather.4
  2234.0 58.1 all-gather.2
  2395.6 42.1 all-gather.4
  2603.5 58.1 all-gather.2
  2764.9 42.1 all-gather.4
  2972.7 58.1 all-gather.2
  3086.4 40.7 reduce-scatter.5
  3134.2 42.1 all-gather.4
  3341.8 58.1 all-gather.2
  3503.4 42.1 all-gather.4
  3711.3 58.1 all-gather.2
  3872.7 42.1 all-gather.4
  (20 shorter events, 811.1 us)
Sparse Core Ops, SparseCore 1:
  4087.7 101.1 reduce-scatter.3
where the time goes:
time: 4210 us; the launch traced here: 4200 us
  waiting for transfers between devices  2100 us (50%)
  matrix products  1490 us (35%)
  other arithmetic  299 us (7%)
  local copies, waits for them, and re-layouts  171 us (4%)
  loops' own time  101 us (2%)
    all_gather x22, waiting for transfers between devices, run_layer(): gathered = lax.all_gather(normed, 'tp', axis=1, tiled=True)  1070 us
    reduce_scatter x22, waiting for transfers between devices, run_layer(): lax.psum_scatter(part_sum, 'tp', scatter_dimension=1, tiled=True)  876 us
    dot_general x11, matrix products, run_layer(): jnp.einsum('btd,df->btf', gathered, w_u, preferred_element_type=jnp.float32)  414 us
    dot_general x11, matrix products, run_layer(): jnp.einsum('btd,df->btf', gathered, w_g, preferred_element_type=jnp.float32)  392 us
    dot_general x11, matrix products, run_layer(): jnp.einsum('btf,fd->btd', hidden, w_d, preferred_element_type=jnp.float32)  382 us
    reduce_scatter x1, waiting for transfers between devices, stage_program(): return lax.psum_scatter(finished, 'pp', scatter_dimension=2, tiled=True)  101 us
    another operation x11, loops' own time, attend(): blocks = lax.map(one_block, starts)  90.6 us
    reduce_sum x44, other arithmetic, rms_scale(): mean_sq = jnp.mean(as_f32 * as_f32, axis=-1, keepdims=True)  88.7 us
  transfers between devices with their start and end apart: 56, of which 56 were waited for; matrix products, arithmetic and copies ran while one was open for 1% of the time, Pallas kernels for 0%

commit v1 on v0

v1 whole, which is shorter than its diff:
```python
import functools

import jax
import jax.numpy as jnp
from jax import lax
from jax.experimental import pallas as pl
from jax.experimental.pallas import tpu as pltpu
from jax.sharding import PartitionSpec as P

WINDOW = 512
SOFTCAP = 50.0
ROPE_BASE = 10000.0
NORM_EPS = 1e-6
MESH = pl.DeviceIdType.MESH

D = 2048
HEAD = 256
HEADS = 8
KV = 2
GROUP = 4
FF_LOCAL = 8192
SEQ = 768
MICRO = 8
STAGES = 4
CHUNK = 192
CHUNKS = SEQ // CHUNK
ROWS = 2 * CHUNK
UNITS = (MICRO // 2) * CHUNKS
GATE_N = 512
GATE_BLOCKS = FF_LOCAL // GATE_N
DOWN_N = 256
DOWN_BLOCKS = D // DOWN_N
RING = 2
STRIP = 32
OUT_ROWS = 96
F32 = jnp.float32
BF16 = jnp.bfloat16


def rope_tables():
    half = HEAD // 2
    frequency = jnp.power(ROPE_BASE, -2.0 * jnp.arange(half, dtype=F32) / HEAD)
    angle = jnp.arange(SEQ, dtype=F32)[:, None] * frequency[None, :]
    return jnp.cos(angle), jnp.sin(angle)


def dot(a, b):
    return jnp.dot(a, b, preferred_element_type=F32)


def kernel(hidden, gains, cos, sin, wq_hbm, wkv_hbm, wo_hbm, wg_hbm, wu_hbm, wd_hbm, out,
           wq, wkv, wo, hid, wg, wu, wd, ubuf, kcache, vcache, xbuf, x1buf, psend, precv, acc,
           qbuf, hbuf, xout,
           load_sem, gq_sem, go_sem, g_sem, d_sem, u_send, u_recv, p_send, p_recv,
           x_recv, x_send, f_send, credit, go, out_recv, out_send, out_local):
    tp = lax.axis_index('tp')
    stage = lax.axis_index('pp')
    other = 1 - tp
    first = stage == 0
    last = stage == STAGES - 1
    odd = stage % 2
    half = HEADS // 2 * HEAD

    def g_copies(index):
        block = lax.rem(index, GATE_BLOCKS)
        slot = lax.rem(index, RING)
        cols = pl.ds(pl.multiple_of(block * GATE_N, GATE_N), GATE_N)
        return (pltpu.make_async_copy(wg_hbm.at[:, cols], wg.at[slot], g_sem.at[0, slot]),
                pltpu.make_async_copy(wu_hbm.at[:, cols], wu.at[slot], g_sem.at[1, slot]))

    def d_copy(index):
        block = lax.rem(index, DOWN_BLOCKS)
        slot = lax.rem(index, RING)
        cols = pl.ds(pl.multiple_of(block * DOWN_N, DOWN_N), DOWN_N)
        return pltpu.make_async_copy(wd_hbm.at[:, cols], wd.at[slot], d_sem.at[slot])

    def feed(unit):
        micro = lax.div(unit, CHUNKS)
        chunk = lax.rem(unit, CHUNKS)
        slot = lax.rem(unit, 2)

        @pl.when(first & (lax.div(chunk, 2) == tp))
        def _():
            rows = pl.ds(pl.multiple_of(lax.rem(chunk, 2) * CHUNK, CHUNK), CHUNK)
            pltpu.make_async_copy(hidden.at[2 * micro + tp, rows, :], xbuf.at[slot], x_recv.at[slot]).start()
            pltpu.make_async_remote_copy(
                hidden.at[2 * micro + other, rows, :], xbuf.at[slot], f_send.at[slot], x_recv.at[slot],
                device_id={'tp': other}, device_id_type=MESH).start()

    def feed_wait(unit):
        chunk = lax.rem(unit, CHUNKS)
        slot = lax.rem(unit, 2)

        @pl.when(first & (lax.div(chunk, 2) == tp))
        def _():
            pltpu.make_async_remote_copy(
                hidden.at[0, pl.ds(0, CHUNK), :], xbuf.at[slot], f_send.at[slot], x_recv.at[slot],
                device_id={'tp': other}, device_id_type=MESH).wait_send()

    gather_q = pltpu.make_async_remote_copy(
        wq_hbm, wq.at[:, pl.ds(pl.multiple_of(tp * half, half), half)], gq_sem.at[0], gq_sem.at[1],
        device_id={'tp': other}, device_id_type=MESH)
    gather_o = pltpu.make_async_remote_copy(
        wo_hbm, wo.at[pl.ds(pl.multiple_of(tp * half, half), half), :], go_sem.at[0], go_sem.at[1],
        device_id={'tp': other}, device_id_type=MESH)
    own_q = pltpu.make_async_copy(wq_hbm, wq.at[:, pl.ds(pl.multiple_of(tp * half, half), half)], load_sem.at[0])
    own_o = pltpu.make_async_copy(wo_hbm, wo.at[pl.ds(pl.multiple_of(tp * half, half), half), :], load_sem.at[1])
    own_kv = pltpu.make_async_copy(wkv_hbm, wkv, load_sem.at[2])

    def u_copy(unit):
        slot = lax.rem(unit, 2)
        return pltpu.make_async_remote_copy(
            ubuf.at[slot, pl.ds(0, CHUNK), :], ubuf.at[slot, pl.ds(CHUNK, CHUNK), :], u_send.at[slot], u_recv.at[slot],
            device_id={'tp': other}, device_id_type=MESH)

    def p_copy(unit, block):
        slot = lax.rem(unit, 2)
        cols = pl.ds(pl.multiple_of(block * DOWN_N, DOWN_N), DOWN_N)
        return pltpu.make_async_remote_copy(
            psend.at[:, cols], precv.at[slot, :, cols], p_send.at[block], p_recv.at[slot, block],
            device_id={'tp': other}, device_id_type=MESH)

    def x_copy(unit):
        slot = lax.rem(unit, 2)
        return pltpu.make_async_remote_copy(
            xout, xbuf.at[slot], x_send.at[slot], x_recv.at[slot],
            device_id={'pp': stage + 1}, device_id_type=MESH)

    def out_parts(unit):
        micro = 2 * lax.div(unit, CHUNKS) + tp
        chunk = lax.rem(unit, CHUNKS)
        to_tp = lax.div(chunk, 2)
        parts = []
        for t in range(2):
            to_pp = lax.rem(chunk, 2) * 2 + t
            here = (to_tp == tp) & (to_pp == STAGES - 1)
            rows = pl.ds(t * OUT_ROWS, OUT_ROWS)
            local = pltpu.make_async_copy(xout.at[rows, :], out.at[micro], out_local)
            remote = pltpu.make_async_remote_copy(
                xout.at[rows, :], out.at[micro], out_send.at[t], out_recv.at[micro],
                device_id={'tp': to_tp, 'pp': to_pp}, device_id_type=MESH)
            parts.append((here, local, remote))
        return parts

    def sends_wait(unit):
        @pl.when(jnp.logical_not(last))
        def _():
            x_copy(unit).wait_send()

        @pl.when(last)
        def _():
            for here, local, remote in out_parts(unit):
                @pl.when(here)
                def _():
                    local.wait()

                @pl.when(jnp.logical_not(here))
                def _():
                    remote.wait_send()

    def normed(values, gain_row):
        mean_sq = jnp.mean(values * values, axis=-1, keepdims=True)
        return (values * lax.rsqrt(mean_sq + NORM_EPS) * (1.0 + gains[pl.ds(gain_row, 1), :])).astype(BF16)

    def attention(chunk, n):
        base = chunk * CHUNK
        row = lax.broadcasted_iota(jnp.int32, (GROUP, CHUNK, n), 1).reshape(GROUP * CHUNK, n) + base
        col = lax.broadcasted_iota(jnp.int32, (GROUP * CHUNK, n), 1)
        offset = row - col
        reach = jnp.where(odd == 0, WINDOW, SEQ)
        allowed = (offset >= 0) & (offset < reach)
        for g in range(KV):
            q = qbuf[pl.ds(g * GROUP, GROUP)].reshape(GROUP * CHUNK, HEAD)
            k = kcache[pl.ds(0, n), g * HEAD:(g + 1) * HEAD]
            v = vcache[pl.ds(0, n), g * HEAD:(g + 1) * HEAD]
            s = lax.dot_general(q, k, (((1,), (1,)), ((), ())), preferred_element_type=F32)
            s = SOFTCAP * jnp.tanh(s * (HEAD ** -0.5 / SOFTCAP))
            e = jnp.where(allowed, jnp.exp(s), 0.0)
            p = (e / jnp.sum(e, axis=-1, keepdims=True)).astype(BF16)
            o = dot(p, v).astype(BF16)
            for h in range(GROUP):
                hbuf[:, (g * GROUP + h) * HEAD:(g * GROUP + h + 1) * HEAD] = o[h * CHUNK:(h + 1) * CHUNK, :]

    def attend(unit):
        chunk = lax.rem(unit, CHUNKS)
        slot = lax.rem(unit, 2)
        pltpu.make_async_copy(xout, xbuf.at[slot], x_recv.at[slot]).wait()

        @pl.loop(0, CHUNK // STRIP)
        def _(r):
            rows = pl.ds(pl.multiple_of(r * STRIP, STRIP), STRIP)
            hbuf[rows, :] = normed(xbuf[slot, rows, :].astype(F32), 0)

        @pl.when(unit == 0)
        def _():
            own_kv.wait()

        positions = pl.ds(pl.multiple_of(chunk * CHUNK, CHUNK), CHUNK)

        def rotated(value):
            a, b = value[:, :HEAD // 2], value[:, HEAD // 2:]
            c, s = cos[positions, :], sin[positions, :]
            return (a * c - b * s).astype(BF16), (b * c + a * s).astype(BF16)

        k = dot(hbuf[...], wkv[:, :KV * HEAD])
        for g in range(KV):
            a, b = rotated(k[:, g * HEAD:(g + 1) * HEAD])
            kcache[positions, g * HEAD:g * HEAD + HEAD // 2] = a
            kcache[positions, g * HEAD + HEAD // 2:(g + 1) * HEAD] = b
        vcache[positions, :] = dot(hbuf[...], wkv[:, KV * HEAD:]).astype(BF16)

        @pl.when(unit == 0)
        def _():
            own_q.wait()
            gather_q.wait()

        @pl.loop(0, HEADS // 2)
        def _(pair):
            q = dot(hbuf[...], wq[:, pl.ds(pl.multiple_of(pair * 2 * HEAD, 2 * HEAD), 2 * HEAD)])
            for t in range(2):
                a, b = rotated(q[:, t * HEAD:(t + 1) * HEAD])
                qbuf[pair * 2 + t, :, :HEAD // 2] = a
                qbuf[pair * 2 + t, :, HEAD // 2:] = b

        for c in range(CHUNKS):
            @pl.when(chunk == c)
            def _():
                attention(c, (c + 1) * CHUNK)

        @pl.when(unit == 0)
        def _():
            own_o.wait()
            gather_o.wait()

            @pl.when(odd == 0)
            def _():
                pl.semaphore_signal(go, 1, device_id={'pp': stage + 1}, device_id_type=MESH)

        @pl.loop(0, D // 512)
        def _(n):
            cols = pl.ds(pl.multiple_of(n * 512, 512), 512)
            acc[:, cols] = dot(hbuf[...], wo[:, cols])

        @pl.when(unit >= 2)
        def _():
            u_copy(unit).wait_send()

        @pl.loop(0, CHUNK // STRIP)
        def _(r):
            rows = pl.ds(pl.multiple_of(r * STRIP, STRIP), STRIP)
            branch = normed(acc[rows, :].astype(BF16).astype(F32), 1)
            x1 = (xbuf[slot, rows, :].astype(F32) + branch.astype(F32)).astype(BF16)
            x1buf[slot, rows, :] = x1
            ubuf[slot, rows, :] = normed(x1.astype(F32), 2)

        u_copy(unit).start()

        @pl.when(jnp.logical_not(first) & (unit < UNITS - 2))
        def _():
            pl.semaphore_signal(credit, 1, device_id={'pp': stage - 1}, device_id_type=MESH)

    def gate_up(unit):
        slot = lax.rem(unit, 2)
        u_copy(unit).wait_recv()

        @pl.when(unit + 2 < UNITS)
        def _():
            feed_wait(unit)
            feed(unit + 2)

        @pl.loop(0, GATE_BLOCKS)
        def _(block):
            index = unit * GATE_BLOCKS + block
            ring = lax.rem(index, RING)
            for copy in g_copies(index):
                copy.wait()
            for t in range(GATE_N // 256):
                sub = slice(t * 256, (t + 1) * 256)
                gate = dot(ubuf[slot], wg[ring, :, sub])
                up = dot(ubuf[slot], wu[ring, :, sub])
                hid[:, pl.ds(pl.multiple_of(block * GATE_N + t * 256, 256), 256)] = (
                    jax.nn.gelu(gate, approximate=True) * up).astype(BF16)

            @pl.when(index + RING < UNITS * GATE_BLOCKS)
            def _():
                for copy in g_copies(index + RING):
                    copy.start()

    def down(unit):
        @pl.loop(0, DOWN_BLOCKS)
        def _(block):
            index = unit * DOWN_BLOCKS + block
            ring = lax.rem(index, RING)
            cols = pl.ds(pl.multiple_of(block * DOWN_N, DOWN_N), DOWN_N)
            d_copy(index).wait()

            @pl.when(unit > 0)
            def _():
                p_copy(unit, block).wait_send()

            part = dot(hid[...], wd[ring])
            psend[:, cols] = part[CHUNK:, :].astype(BF16)
            acc[:, cols] = part[:CHUNK, :]
            p_copy(unit, block).start()

            @pl.when(index + RING < UNITS * DOWN_BLOCKS)
            def _():
                d_copy(index + RING).start()

    def finish(unit):
        slot = lax.rem(unit, 2)

        @pl.when(unit > 0)
        def _():
            sends_wait(unit - 1)

        @pl.loop(0, DOWN_BLOCKS)
        def _(block):
            p_copy(unit, block).wait_recv()

        @pl.loop(0, CHUNK // STRIP)
        def _(r):
            rows = pl.ds(pl.multiple_of(r * STRIP, STRIP), STRIP)
            total = (acc[rows, :] + precv[slot, rows, :].astype(F32)).astype(BF16)
            branch = normed(total.astype(F32), 3)
            xout[rows, :] = (x1buf[slot, rows, :].astype(F32) + branch.astype(F32)).astype(BF16)

        @pl.when(jnp.logical_not(last))
        def _():
            @pl.when(unit >= 2)
            def _():
                pl.semaphore_wait(credit, 1)
            x_copy(unit).start()

        @pl.when(last)
        def _():
            for here, local, remote in out_parts(unit):
                @pl.when(here)
                def _():
                    local.start()

                @pl.when(jnp.logical_not(here))
                def _():
                    remote.start()

    feed(0)
    own_kv.start()
    own_q.start()
    own_o.start()

    @pl.when(odd == 1)
    def _():
        pl.semaphore_wait(go, 1)

    gather_q.start()
    gather_o.start()
    feed(1)
    for s in range(RING):
        for copy in g_copies(s):
            copy.start()
        d_copy(s).start()

    attend(0)

    @pl.loop(0, UNITS)
    def _(unit):
        gate_up(unit)

        @pl.when(unit + 1 < UNITS)
        def _():
            attend(unit + 1)

        down(unit)
        finish(unit)

    sends_wait(UNITS - 1)
    feed_wait(UNITS - 2)
    feed_wait(UNITS - 1)
    for s in range(2):
        u_copy(UNITS - 2 + s).wait_send()

    @pl.loop(0, DOWN_BLOCKS)
    def _(block):
        p_copy(UNITS - 1, block).wait_send()

    for m in range(MICRO):
        @pl.when(jnp.logical_not(last & (tp == m % 2)))
        def _():
            pltpu.make_async_copy(xout.at[pl.ds(0, OUT_ROWS), :], out.at[m], out_recv.at[m]).wait()


def solution(mesh):
    in_specs = (P('dp', None, 'tp', None), P('pp', None, None), P('pp', None, 'tp', None),
                P('pp', None, None, None), P('pp', None, None, None), P('pp', 'tp', None, None),
                P('pp', None, 'tp'), P('pp', None, 'tp'), P('pp', 'tp', None))
    out_spec = P('dp', None, ('tp', 'pp'), None)

    def stage_program(hidden_in, norm_gains, w_query, w_key, w_value, w_out, w_gate, w_up, w_down):
        cos, sin = rope_tables()
        wq = w_query[0].reshape(D, HEADS // 2 * HEAD)
        wkv = jnp.concatenate([w_key[0].reshape(D, KV * HEAD), w_value[0].reshape(D, KV * HEAD)], axis=1)
        wo = w_out[0].reshape(HEADS // 2 * HEAD, D)
        hbm = pl.BlockSpec(memory_space=pl.ANY)
        vmem = pl.BlockSpec(memory_space=pltpu.VMEM)
        dma = pltpu.SemaphoreType.DMA
        out = pl.pallas_call(
            kernel,
            out_shape=jax.ShapeDtypeStruct((MICRO, OUT_ROWS, D), BF16),
            in_specs=[hbm, vmem, vmem, vmem] + [hbm] * 6,
            out_specs=hbm,
            scratch_shapes=[
                pltpu.VMEM((D, HEADS * HEAD), BF16),
                pltpu.VMEM((D, 2 * KV * HEAD), BF16),
                pltpu.VMEM((HEADS * HEAD, D), BF16),
                pltpu.VMEM((ROWS, FF_LOCAL), BF16),
                pltpu.VMEM((RING, D, GATE_N), BF16),
                pltpu.VMEM((RING, D, GATE_N), BF16),
                pltpu.VMEM((RING, FF_LOCAL, DOWN_N), BF16),
                pltpu.VMEM((2, ROWS, D), BF16),
                pltpu.VMEM((SEQ, KV * HEAD), BF16),
                pltpu.VMEM((SEQ, KV * HEAD), BF16),
                pltpu.VMEM((2, CHUNK, D), BF16),
                pltpu.VMEM((2, CHUNK, D), BF16),
                pltpu.VMEM((CHUNK, D), BF16),
                pltpu.VMEM((2, CHUNK, D), BF16),
                pltpu.VMEM((CHUNK, D), F32),
                pltpu.VMEM((HEADS, CHUNK, HEAD), BF16),
                pltpu.VMEM((CHUNK, D), BF16),
                pltpu.VMEM((CHUNK, D), BF16),
                dma((3,)), dma((2,)), dma((2,)), dma((2, RING)), dma((RING,)), dma((2,)), dma((2,)),
                dma((DOWN_BLOCKS,)), dma((2, DOWN_BLOCKS)), dma((2,)), dma((2,)), dma((2,)),
                pltpu.SemaphoreType.REGULAR, pltpu.SemaphoreType.REGULAR,
                dma((MICRO,)), dma((2,)), dma,
            ],
            compiler_params=pltpu.CompilerParams(has_side_effects=True, vmem_limit_bytes=67043328),
            name='pipeline',
        )(hidden_in.reshape(MICRO, SEQ // 2, D), norm_gains[0], cos, sin, wq, wkv, wo, w_gate[0], w_up[0], w_down[0])
        return out.reshape(MICRO, 1, OUT_ROWS, D)

    return jax.shard_map(stage_program, mesh=mesh, in_specs=in_specs, out_specs=out_spec, check_vma=False)
```

time: 4210 us -> 1470 us (0.35)
  waiting for transfers between devices: 2100 us -> 0 us
  matrix products: 1490 us -> 0 us
  Pallas kernels: 0 us -> 1450 us
  other arithmetic: 299 us -> 5.04 us
  local copies, waits for them, and re-layouts: 171 us -> 10.4 us
  loops' own time: 101 us -> 0 us
    dot_general x143 -> x0, matrix products: 1490 us -> none  [the longest x11 414 us: run_layer(): jnp.einsum('btd,df->btf', gathered, w_u, preferred_element_type=jnp.float32)]
    pallas_call x0 -> x1, Pallas kernels: none -> 1450 us  [stage_program(): pl.pallas_call(kernel, out_shape=jax.ShapeDtypeStruct((MICRO, OUT_ROWS, D...]
    all_gather x22 -> x0, waiting for transfers between devices: 1070 us -> none  [run_layer(): gathered = lax.all_gather(normed, 'tp', axis=1, tiled=True)]
    reduce_scatter x23 -> x0, waiting for transfers between devices: 977 us -> none  [the longest x22 876 us: run_layer(): lax.psum_scatter(part_sum, 'tp', scatter_dimension=1, tiled=True)]
    reduce_sum x77 -> x0, other arithmetic: 122 us -> none  [the longest x44 88.7 us: rms_scale(): mean_sq = jnp.mean(as_f32 * as_f32, axis=-1, keepdims=True)]
    another operation x23 -> x0, loops' own time: 101 us -> none  [the longest x11 90.6 us: attend(): blocks = lax.map(one_block, starts)]
    dynamic_slice x45 -> x0, local copies, waits for them, and re-layouts: 67 us -> none  [the longest x33 43.4 us: attend(): blocks = lax.map(one_block, starts)]
    dynamic_update_slice x11 -> x0, other arithmetic: 49.2 us -> none  [step_body(): lax.dynamic_update_slice_in_dim(out_buf, stored[None], slot, axis=0)]
  transfers between devices with their start and end apart: 56 -> 0, of which waited for: 56 -> 0; matrix products, arithmetic and copies ran while one was open for 1% -> 0% of each run, Pallas kernels for 0% -> 0%
where the time goes in v1:
time: 1470 us
  Pallas kernels  1450 us (99%)
    pallas_call x1, Pallas kernels, stage_program(): pl.pallas_call(kernel, out_shape=jax.ShapeDtypeStruct((MICRO, OUT_ROWS, D...  1450 us

profile of v1, /device:TPU:7, one launch (start us, length us, event | category | flops | bytes accessed | tf_op | source)
XLA Modules:
  0.0 1469.2 jit_solution(6960538878516217738)
XLA Ops:
  0.0 0.0 copy-start.1
  0.0 2.3 fusion
  2.3 2.0 copy.12
  4.3 0.0 copy-done.1
  4.3 0.5 copy.13
  4.9 0.0 copy-start
  4.9 2.8 pad_maximum_fusion.wkv_hbm
  7.6 0.9 copy-done
  8.5 3.0 copy.11
  11.5 1453.7 %pipeline.1 = bf16[8,96,2048]{2,1,0:T(8,128)(2,1)} custom-call(bf16[8,384,2048]{2,1,0:T(8,128)(2,1)} %bitcast.22, f32[4,2048]{1,0:T(4,128)} %bitcast.30, f32[768,128]{1,0:T(8,128)} %get-tuple-element.6.cos, f32[768,128]{1,0:T(8,128)} %get-tuple-element.5.sin, bf16[2048,1024]{1,0:T(8,128)(2,1)} %bitcast.21, bf16[2048,1024]{1,0:T(8,128)(2,1)} %pad_maximum_fusion.wkv_hbm, ...), custom_call_target="tpu_custom_call" | custom-call | tf_op jit(solution)/shard_map/pipeline/pallas_call | solution.py:406
  1465.2 4.0 copy.15
  (1 shorter events, 0.0 us)
Async XLA Ops:
  0.0 4.3 copy-start.1
  4.9 3.6 copy-start

commit v2 on v1

--- a/solution.py
+++ b/solution.py
@@ -28,11 +28,15 @@
 UNITS = (MICRO // 2) * CHUNKS
 GATE_N = 512
 GATE_BLOCKS = FF_LOCAL // GATE_N
-DOWN_N = 256
+DOWN_N = 512
 DOWN_BLOCKS = D // DOWN_N
-RING = 2
-STRIP = 32
+DOWN_K = FF_LOCAL // D
+RING = 8
+FINISH_AT = 4
+ATTEND_AT = 8
+STRIP = 64
 OUT_ROWS = 96
+PIECES = 8
 F32 = jnp.float32
 BF16 = jnp.bfloat16
 
@@ -49,9 +53,9 @@
 
 
 def kernel(hidden, gains, cos, sin, wq_hbm, wkv_hbm, wo_hbm, wg_hbm, wu_hbm, wd_hbm, out,
-           wq, wkv, wo, hid, wg, wu, wd, ubuf, kcache, vcache, xbuf, x1buf, psend, precv, acc,
+           wq, wkv, wo, hid, ring, ubuf, kcache, vcache, xbuf, x1buf, psend, precv, acc,
            qbuf, hbuf, xout,
-           load_sem, gq_sem, go_sem, g_sem, d_sem, u_send, u_recv, p_send, p_recv,
+           load_sem, gq_sem, go_sem, relay_send, relay_recv, back_send, back_recv, ready, ring_sem, u_send, u_recv, p_send, p_recv,
            x_recv, x_send, f_send, credit, go, out_recv, out_send, out_local):
     tp = lax.axis_index('tp')
     stage = lax.axis_index('pp')
@@ -60,19 +64,21 @@
     last = stage == STAGES - 1
     odd = stage % 2
     half = HEADS // 2 * HEAD
-
-    def g_copies(index):
-        block = lax.rem(index, GATE_BLOCKS)
-        slot = lax.rem(index, RING)
+    west = stage < STAGES // 2
+    piece = half // PIECES
+
+    def gate_copies(block):
+        slot = 2 * lax.rem(block, RING // 2)
         cols = pl.ds(pl.multiple_of(block * GATE_N, GATE_N), GATE_N)
-        return (pltpu.make_async_copy(wg_hbm.at[:, cols], wg.at[slot], g_sem.at[0, slot]),
-                pltpu.make_async_copy(wu_hbm.at[:, cols], wu.at[slot], g_sem.at[1, slot]))
-
-    def d_copy(index):
-        block = lax.rem(index, DOWN_BLOCKS)
-        slot = lax.rem(index, RING)
+        return (pltpu.make_async_copy(wg_hbm.at[:, cols], ring.at[slot], ring_sem.at[slot]),
+                pltpu.make_async_copy(wu_hbm.at[:, cols], ring.at[slot + 1], ring_sem.at[slot + 1]))
+
+    def down_copies(block, parts):
+        slot = DOWN_K * lax.rem(block, RING // DOWN_K)
         cols = pl.ds(pl.multiple_of(block * DOWN_N, DOWN_N), DOWN_N)
-        return pltpu.make_async_copy(wd_hbm.at[:, cols], wd.at[slot], d_sem.at[slot])
+        return [pltpu.make_async_copy(
+            wd_hbm.at[pl.ds(part * D if isinstance(part, int) else pl.multiple_of(part * D, D), D), cols],
+            ring.at[slot + part], ring_sem.at[slot + part]) for part in parts]
 
     def feed(unit):
         micro = lax.div(unit, CHUNKS)
@@ -106,6 +112,37 @@
     own_q = pltpu.make_async_copy(wq_hbm, wq.at[:, pl.ds(pl.multiple_of(tp * half, half), half)], load_sem.at[0])
     own_o = pltpu.make_async_copy(wo_hbm, wo.at[pl.ds(pl.multiple_of(tp * half, half), half), :], load_sem.at[1])
     own_kv = pltpu.make_async_copy(wkv_hbm, wkv, load_sem.at[2])
+
+    def relay_out(p):
+        rows = pl.ds(pl.multiple_of(p * piece, piece), piece)
+        there = pl.ds(pl.multiple_of(tp * half + p * piece, piece), piece)
+        return pltpu.make_async_remote_copy(
+            wo_hbm.at[rows, :], wo.at[there, :], relay_send.at[p], relay_recv.at[p],
+            device_id={'tp': other, 'pp': stage + STAGES // 2}, device_id_type=MESH)
+
+    def relay_back(p):
+        rows = pl.ds(pl.multiple_of(other * half + p * piece, piece), piece)
+        return pltpu.make_async_remote_copy(
+            wo.at[rows, :], wo.at[rows, :], back_send.at[p], back_recv.at[p],
+            device_id={'pp': stage - STAGES // 2}, device_id_type=MESH)
+
+    def gather_o_wait():
+        own_o.wait()
+
+        @pl.when(west)
+        def _():
+            @pl.loop(0, PIECES)
+            def _(p):
+                relay_out(p).wait_send()
+                relay_back(p).wait_recv()
+
+        @pl.when(jnp.logical_not(west))
+        def _():
+            gather_o.wait()
+
+        @pl.when(odd == 0)
+        def _():
+            pl.semaphore_signal(go, 1, device_id={'pp': stage + 1}, device_id_type=MESH)
 
     def u_copy(unit):
         slot = lax.rem(unit, 2)
@@ -202,43 +239,39 @@
             c, s = cos[positions, :], sin[positions, :]
             return (a * c - b * s).astype(BF16), (b * c + a * s).astype(BF16)
 
-        k = dot(hbuf[...], wkv[:, :KV * HEAD])
+        kv = dot(hbuf[...], wkv[...])
+        k = kv[:, :KV * HEAD]
         for g in range(KV):
             a, b = rotated(k[:, g * HEAD:(g + 1) * HEAD])
             kcache[positions, g * HEAD:g * HEAD + HEAD // 2] = a
             kcache[positions, g * HEAD + HEAD // 2:(g + 1) * HEAD] = b
-        vcache[positions, :] = dot(hbuf[...], wkv[:, KV * HEAD:]).astype(BF16)
-
-        @pl.when(unit == 0)
+        vcache[positions, :] = kv[:, KV * HEAD:].astype(BF16)
+
+        @pl.when(first & (unit == 0))
         def _():
             own_q.wait()
             gather_q.wait()
 
-        @pl.loop(0, HEADS // 2)
-        def _(pair):
-            q = dot(hbuf[...], wq[:, pl.ds(pl.multiple_of(pair * 2 * HEAD, 2 * HEAD), 2 * HEAD)])
-            for t in range(2):
+        @pl.loop(0, KV)
+        def _(g):
+            q = dot(hbuf[...], wq[:, pl.ds(pl.multiple_of(g * GROUP * HEAD, GROUP * HEAD), GROUP * HEAD)])
+            for t in range(GROUP):
                 a, b = rotated(q[:, t * HEAD:(t + 1) * HEAD])
-                qbuf[pair * 2 + t, :, :HEAD // 2] = a
-                qbuf[pair * 2 + t, :, HEAD // 2:] = b
+                qbuf[g * GROUP + t, :, :HEAD // 2] = a
+                qbuf[g * GROUP + t, :, HEAD // 2:] = b
 
         for c in range(CHUNKS):
             @pl.when(chunk == c)
             def _():
                 attention(c, (c + 1) * CHUNK)
 
-        @pl.when(unit == 0)
-        def _():
-            own_o.wait()
-            gather_o.wait()
-
-            @pl.when(odd == 0)
-            def _():
-                pl.semaphore_signal(go, 1, device_id={'pp': stage + 1}, device_id_type=MESH)
-
-        @pl.loop(0, D // 512)
+        @pl.when(first & (unit == 0))
+        def _():
+            gather_o_wait()
+
+        @pl.loop(0, D // 1024)
         def _(n):
-            cols = pl.ds(pl.multiple_of(n * 512, 512), 512)
+            cols = pl.ds(pl.multiple_of(n * 1024, 1024), 1024)
             acc[:, cols] = dot(hbuf[...], wo[:, cols])
 
         @pl.when(unit >= 2)
@@ -259,53 +292,61 @@
         def _():
             pl.semaphore_signal(credit, 1, device_id={'pp': stage - 1}, device_id_type=MESH)
 
-    def gate_up(unit):
-        slot = lax.rem(unit, 2)
-        u_copy(unit).wait_recv()
-
-        @pl.when(unit + 2 < UNITS)
-        def _():
-            feed_wait(unit)
-            feed(unit + 2)
-
-        @pl.loop(0, GATE_BLOCKS)
+    def gate_up(unit, begin, end):
+        slot = lax.rem(unit, 2)
+
+        @pl.loop(begin, end)
         def _(block):
-            index = unit * GATE_BLOCKS + block
-            ring = lax.rem(index, RING)
-            for copy in g_copies(index):
+            for copy in gate_copies(block):
                 copy.wait()
-            for t in range(GATE_N // 256):
-                sub = slice(t * 256, (t + 1) * 256)
-                gate = dot(ubuf[slot], wg[ring, :, sub])
-                up = dot(ubuf[slot], wu[ring, :, sub])
-                hid[:, pl.ds(pl.multiple_of(block * GATE_N + t * 256, 256), 256)] = (
-                    jax.nn.gelu(gate, approximate=True) * up).astype(BF16)
-
-            @pl.when(index + RING < UNITS * GATE_BLOCKS)
-            def _():
-                for copy in g_copies(index + RING):
+            at = 2 * lax.rem(block, RING // 2)
+            gate = dot(ubuf[slot], ring[at])
+            up = dot(ubuf[slot], ring[at + 1])
+            hid[:, pl.ds(pl.multiple_of(block * GATE_N, GATE_N), GATE_N)] = (
+                jax.nn.gelu(gate, approximate=True) * up).astype(BF16)
+            ahead = block + RING // 2
+
+            @pl.when(ahead < GATE_BLOCKS)
+            def _():
+                for copy in gate_copies(ahead):
+                    copy.start()
+
+            @pl.when(ahead >= GATE_BLOCKS)
+            def _():
+                over = ahead - GATE_BLOCKS
+                for copy in down_copies(lax.div(over, 2), [2 * lax.rem(over, 2), 2 * lax.rem(over, 2) + 1]):
                     copy.start()
 
     def down(unit):
         @pl.loop(0, DOWN_BLOCKS)
         def _(block):
-            index = unit * DOWN_BLOCKS + block
-            ring = lax.rem(index, RING)
             cols = pl.ds(pl.multiple_of(block * DOWN_N, DOWN_N), DOWN_N)
-            d_copy(index).wait()
+            at = DOWN_K * lax.rem(block, RING // DOWN_K)
 
             @pl.when(unit > 0)
             def _():
                 p_copy(unit, block).wait_send()
 
-            part = dot(hid[...], wd[ring])
+            for copy in down_copies(block, range(DOWN_K)):
+                copy.wait()
+            part = dot(hid[:, :D], ring[at])
+            for k in range(1, DOWN_K):
+                part = part + dot(hid[:, k * D:(k + 1) * D], ring[at + k])
             psend[:, cols] = part[CHUNK:, :].astype(BF16)
             acc[:, cols] = part[:CHUNK, :]
             p_copy(unit, block).start()
-
-            @pl.when(index + RING < UNITS * DOWN_BLOCKS)
-            def _():
-                d_copy(index + RING).start()
+            ahead = block + RING // DOWN_K
+
+            @pl.when(ahead < DOWN_BLOCKS)
+            def _():
+                for copy in down_copies(ahead, range(DOWN_K)):
+                    copy.start()
+
+            @pl.when((ahead >= DOWN_BLOCKS) & (unit + 1 < UNITS))
+            def _():
+                for t in range(2):
+                    for copy in gate_copies((ahead - DOWN_BLOCKS) * 2 + t):
+                        copy.start()
 
     def finish(unit):
         slot = lax.rem(unit, 2)
@@ -348,31 +389,77 @@
     own_q.start()
     own_o.start()
 
-    @pl.when(odd == 1)
+    for s in range(RING // 2):
+        for copy in gate_copies(s):
+            copy.start()
+
+    @pl.when(west)
     def _():
-        pl.semaphore_wait(go, 1)
-
-    gather_q.start()
-    gather_o.start()
+        @pl.when(odd == 1)
+        def _():
+            pl.semaphore_wait(go, 1)
+
+        gather_q.start()
+
+        @pl.loop(0, PIECES)
+        def _(p):
+            relay_out(p).start()
+
+    @pl.when(jnp.logical_not(west))
+    def _():
+        @pl.loop(0, PIECES)
+        def _(p):
+            relay_out(p).wait_recv()
+            relay_back(p).start()
+
+        @pl.loop(0, PIECES)
+        def _(p):
+            relay_back(p).wait_send()
+
+        pl.semaphore_signal(ready, 1, device_id={'tp': other}, device_id_type=MESH)
+        pl.semaphore_wait(ready, 1)
+
+        @pl.when(odd == 1)
+        def _():
+            pl.semaphore_wait(go, 1)
+
+        gather_q.start()
+        gather_o.start()
+
+    @pl.when(jnp.logical_not(first))
+    def _():
+        own_q.wait()
+        gather_q.wait()
+        gather_o_wait()
+
     feed(1)
-    for s in range(RING):
-        for copy in g_copies(s):
-            copy.start()
-        d_copy(s).start()
-
     attend(0)
 
     @pl.loop(0, UNITS)
     def _(unit):
-        gate_up(unit)
+        u_copy(unit).wait_recv()
+
+        @pl.when(unit + 2 < UNITS)
+        def _():
+            feed_wait(unit)
+            feed(unit + 2)
+
+        gate_up(unit, 0, FINISH_AT)
+
+        @pl.when(unit > 0)
+        def _():
+            finish(unit - 1)
+
+        gate_up(unit, FINISH_AT, ATTEND_AT)
 
         @pl.when(unit + 1 < UNITS)
         def _():
             attend(unit + 1)
 
+        gate_up(unit, ATTEND_AT, GATE_BLOCKS)
         down(unit)
-        finish(unit)
-
+
+    finish(UNITS - 1)
     sends_wait(UNITS - 1)
     feed_wait(UNITS - 2)
     feed_wait(UNITS - 1)
@@ -414,8 +501,6 @@
                 pltpu.VMEM((HEADS * HEAD, D), BF16),
                 pltpu.VMEM((ROWS, FF_LOCAL), BF16),
                 pltpu.VMEM((RING, D, GATE_N), BF16),
-                pltpu.VMEM((RING, D, GATE_N), BF16),
-                pltpu.VMEM((RING, FF_LOCAL, DOWN_N), BF16),
                 pltpu.VMEM((2, ROWS, D), BF16),
                 pltpu.VMEM((SEQ, KV * HEAD), BF16),
                 pltpu.VMEM((SEQ, KV * HEAD), BF16),
@@ -427,7 +512,8 @@
                 pltpu.VMEM((HEADS, CHUNK, HEAD), BF16),
                 pltpu.VMEM((CHUNK, D), BF16),
                 pltpu.VMEM((CHUNK, D), BF16),
-                dma((3,)), dma((2,)), dma((2,)), dma((2, RING)), dma((RING,)), dma((2,)), dma((2,)),
+                dma((3,)), dma((2,)), dma((2,)),
+                dma((PIECES,)), dma((PIECES,)), dma((PIECES,)), dma((PIECES,)), pltpu.SemaphoreType.REGULAR, dma((RING,)), dma((2,)), dma((2,)),
                 dma((DOWN_BLOCKS,)), dma((2, DOWN_BLOCKS)), dma((2,)), dma((2,)), dma((2,)),
                 pltpu.SemaphoreType.REGULAR, pltpu.SemaphoreType.REGULAR,
                 dma((MICRO,)), dma((2,)), dma,

time: 1470 us -> 1250 us (0.85)
  Pallas kernels: 1450 us -> 1230 us
    pallas_call x1, Pallas kernels: 1450 us -> 1230 us  [stage_program(): pl.pallas_call(kernel, out_shape=jax.ShapeDtypeStruct((MICRO, OUT_ROWS, D...]
where the time goes in v2:
time: 1250 us
  Pallas kernels  1230 us (98%)
    pallas_call x1, Pallas kernels, stage_program(): pl.pallas_call(kernel, out_shape=jax.ShapeDtypeStruct((MICRO, OUT_ROWS, D...  1230 us

profile of v2, /device:TPU:7, one launch (start us, length us, event | category | flops | bytes accessed | tf_op | source)
XLA Modules:
  0.0 1249.5 jit_solution(5556802413648775712)
XLA Ops:
  0.0 0.0 copy-start.1
  0.0 2.3 fusion
  2.3 2.0 copy.12
  4.3 0.0 copy-done.1
  4.3 0.5 copy.13
  4.9 0.0 copy-start
  4.9 2.8 pad_maximum_fusion.wkv_hbm
  7.6 0.9 copy-done
  8.5 3.0 copy.11
  11.5 1234.0 %pipeline.1 = bf16[8,96,2048]{2,1,0:T(8,128)(2,1)} custom-call(bf16[8,384,2048]{2,1,0:T(8,128)(2,1)} %bitcast.22, f32[4,2048]{1,0:T(4,128)} %bitcast.30, f32[768,128]{1,0:T(8,128)} %get-tuple-element.6.cos, f32[768,128]{1,0:T(8,128)} %get-tuple-element.5.sin, bf16[2048,1024]{1,0:T(8,128)(2,1)} %bitcast.21, bf16[2048,1024]{1,0:T(8,128)(2,1)} %pad_maximum_fusion.wkv_hbm, ...), custom_call_target="tpu_custom_call" | custom-call | tf_op jit(solution)/shard_map/pipeline/pallas_call | solution.py:493
  1245.5 4.0 copy.15
  (1 shorter events, 0.0 us)
Async XLA Ops:
  0.0 4.3 copy-start.1
  4.9 3.6 copy-start

commit v3 on v2

--- a/solution.py
+++ b/solution.py
@@ -292,30 +292,29 @@
         def _():
             pl.semaphore_signal(credit, 1, device_id={'pp': stage - 1}, device_id_type=MESH)
 
-    def gate_up(unit, begin, end):
-        slot = lax.rem(unit, 2)
-
-        @pl.loop(begin, end)
-        def _(block):
-            for copy in gate_copies(block):
+    def gate_up(unit, pair):
+        slot = lax.rem(unit, 2)
+        at = 4 * lax.rem(pair, RING // 4)
+        for t in range(2):
+            for copy in gate_copies(2 * pair + t):
                 copy.wait()
-            at = 2 * lax.rem(block, RING // 2)
-            gate = dot(ubuf[slot], ring[at])
-            up = dot(ubuf[slot], ring[at + 1])
-            hid[:, pl.ds(pl.multiple_of(block * GATE_N, GATE_N), GATE_N)] = (
-                jax.nn.gelu(gate, approximate=True) * up).astype(BF16)
-            ahead = block + RING // 2
-
-            @pl.when(ahead < GATE_BLOCKS)
-            def _():
-                for copy in gate_copies(ahead):
+        for t in range(2):
+            gate = dot(ubuf[slot], ring[at + 2 * t])
+            up = dot(ubuf[slot], ring[at + 2 * t + 1])
+            cols = pl.ds(pl.multiple_of((2 * pair + t) * GATE_N, GATE_N), GATE_N)
+            hid[:, cols] = (jax.nn.gelu(gate, approximate=True) * up).astype(BF16)
+        ahead = pair + RING // 4
+
+        @pl.when(ahead < GATE_BLOCKS // 2)
+        def _():
+            for t in range(2):
+                for copy in gate_copies(2 * ahead + t):
                     copy.start()
 
-            @pl.when(ahead >= GATE_BLOCKS)
-            def _():
-                over = ahead - GATE_BLOCKS
-                for copy in down_copies(lax.div(over, 2), [2 * lax.rem(over, 2), 2 * lax.rem(over, 2) + 1]):
-                    copy.start()
+        @pl.when(ahead >= GATE_BLOCKS // 2)
+        def _():
+            for copy in down_copies(ahead - GATE_BLOCKS // 2, range(DOWN_K)):
+                copy.start()
 
     def down(unit):
         @pl.loop(0, DOWN_BLOCKS)
@@ -444,19 +443,18 @@
             feed_wait(unit)
             feed(unit + 2)
 
-        gate_up(unit, 0, FINISH_AT)
-
-        @pl.when(unit > 0)
-        def _():
-            finish(unit - 1)
-
-        gate_up(unit, FINISH_AT, ATTEND_AT)
-
-        @pl.when(unit + 1 < UNITS)
-        def _():
-            attend(unit + 1)
-
-        gate_up(unit, ATTEND_AT, GATE_BLOCKS)
+        @pl.loop(0, GATE_BLOCKS // 2)
+        def _(pair):
+            @pl.when((2 * pair == FINISH_AT) & (unit > 0))
+            def _():
+                finish(unit - 1)
+
+            @pl.when((2 * pair == ATTEND_AT) & (unit + 1 < UNITS))
+            def _():
+                attend(unit + 1)
+
+            gate_up(unit, pair)
+
         down(unit)
 
     finish(UNITS - 1)

time: 1250 us -> 1240 us (level)
  no operation moved by 1% of the time
where the time goes in v3:
time: 1240 us
  Pallas kernels  1230 us (99%)
    pallas_call x1, Pallas kernels, stage_program(): pl.pallas_call(kernel, out_shape=jax.ShapeDtypeStruct((MICRO, OUT_ROWS, D...  1230 us

profile of v3, /device:TPU:7, one launch (start us, length us, event | category | flops | bytes accessed | tf_op | source)
XLA Modules:
  0.0 1242.5 jit_solution(3366650341774418176)
XLA Ops:
  0.0 0.0 copy-start.1
  0.0 2.3 fusion
  2.3 2.0 copy.12
  4.3 0.0 copy-done.1
  4.3 0.5 copy.13
  4.9 0.0 copy-start
  4.9 2.8 pad_maximum_fusion.wkv_hbm
  7.6 0.9 copy-done
  8.5 3.0 copy.11
  11.5 1227.0 %pipeline.1 = bf16[8,96,2048]{2,1,0:T(8,128)(2,1)} custom-call(bf16[8,384,2048]{2,1,0:T(8,128)(2,1)} %bitcast.22, f32[4,2048]{1,0:T(4,128)} %bitcast.30, f32[768,128]{1,0:T(8,128)} %get-tuple-element.6.cos, f32[768,128]{1,0:T(8,128)} %get-tuple-element.5.sin, bf16[2048,1024]{1,0:T(8,128)(2,1)} %bitcast.21, bf16[2048,1024]{1,0:T(8,128)(2,1)} %pad_maximum_fusion.wkv_hbm, ...), custom_call_target="tpu_custom_call" | custom-call | tf_op jit(solution)/shard_map/pipeline/pallas_call | solution.py:491
  1238.5 4.0 copy.15
  (1 shorter events, 0.0 us)
Async XLA Ops:
  0.0 4.3 copy-start.1
  4.9 3.6 copy-start
